TPU v7x, 128 devices: a whole 4x4x4 slice. The times are simulated.
128 devices in a mesh: row: 16 (over x_hi, y, core), col: 4 (over z), dp: 2 (over x_lo).
Axes of the slice: x: 4 (x_hi: 2, x_lo: 2; x = x_hi * 2 + x_lo), y: 4, z: 4, core: 2. Of those that a mesh axis runs over, the one named last changes fastest.
Arguments:
- slides: bfloat16 [2, 256, 128, 512], P('dp', 'row', 'col'), may hold values from -6 to 6
- cotangent: bfloat16 [2, 256, 128, 512], P('dp', 'row', 'col'), may hold values from -6 to 6
- kernel: float32 [2, 7, 7, 512], replicated, may hold values from -0.875 to 0.875
- kernel_bias: float32 [2, 512], replicated, may hold values from -3 to 3
- norm_gain: float32 [2, 512], replicated, may hold values from 0.1 to 1.9
- norm_bias: float32 [2, 512], replicated, may hold values from -3 to 3
- weight_in: bfloat16 [2, 512, 2048], P(None, 'dp'), may hold values from -0.25 to 0.25
- bias_in: float32 [2, 2048], replicated, may hold values from -3 to 3
- weight_out: bfloat16 [2, 2048, 512], P(None, None, 'dp'), may hold values from -0.125 to 0.125
- bias_out: float32 [2, 512], replicated, may hold values from -3 to 3
- layer_scale: float32 [2, 512], replicated, may hold values from 0.3 to 1.5
Outputs:
- output: bfloat16 [2, 256, 128, 512], P('dp', 'row', 'col')
- grad_slides: bfloat16 [2, 256, 128, 512], P('dp', 'row', 'col')
- grad_weight_in: float32 [2, 512, 2048], P(None, 'dp')
- grad_weight_out: float32 [2, 2048, 512], P(None, None, 'dp')
- grad_kernel: float32 [2, 7, 7, 512], replicated
- grad_channel: float32 [2, 5, 512], replicated
- grad_bias_in: float32 [2, 2048], replicated
All inputs are finite; a program needn't handle non-finite values.
Results may differ from a plain program's by a relative error of at most 0.01.
Values may be sent and summed in bfloat16 or wider, within the bound.
No kernel may reach another device: no remote copies, remote signals or barrier semaphores. Data moves between devices by JAX's collectives and lax.ppermute only.
A program may use at most 128 MiB of HBM per device.

v0:
```python
import jax
import jax.numpy as jnp
from jax import lax
from jax.sharding import PartitionSpec as P

COEF = 0.7978845608028654
CUBIC = 0.044715
EPSILON = 1e-06
SPACE = ("xh", "y", "z")
HALF = 1024


def chips_along_x(step):

    def target(pos):
        x = (pos + step) % 4
        return x

    return [(pos, target(pos)) for pos in range(4)]


def swapped(value, axis):
    return lax.ppermute(value, axis, [(0, 1), (1, 0)])


def fetch_weights(own_in, own_out):
    core = lax.axis_index("core")
    part = lax.axis_index("dp")
    send_in = lax.dynamic_slice_in_dim(own_in, core * 128, 128, 0)
    send_out = lax.dynamic_slice_in_dim(own_out, core * 1024, 1024, 0)
    got_in = lax.ppermute(send_in, ("xh", "dp"), chips_along_x(1))
    got_out = lax.ppermute(send_out, ("xh", "dp"), chips_along_x(-1))
    mate_in = swapped(got_in, "core")
    mate_out = swapped(got_out, "core")
    first = core == 0
    other_in = jnp.concatenate(
        [jnp.where(first, got_in, mate_in), jnp.where(first, mate_in, got_in)], 0
    )
    other_out = jnp.concatenate(
        [jnp.where(first, got_out, mate_out), jnp.where(first, mate_out, got_out)], 0
    )
    low = part == 0
    full_in = jnp.concatenate(
        [jnp.where(low, own_in, other_in), jnp.where(low, other_in, own_in)], 0
    )
    full_out = jnp.concatenate(
        [jnp.where(low, own_out, other_out), jnp.where(low, other_out, own_out)], 1
    )
    return (full_in, full_out)


def with_halo(block, sides, width):
    for axis, dim in sides:
        count = lax.axis_size(axis)
        forward = [(i, i + 1) for i in range(count - 1)]
        backward = [(target, source) for source, target in forward]
        low = lax.ppermute(
            lax.slice_in_dim(block, block.shape[dim] - width, None, axis=dim), axis, forward
        )
        high = lax.ppermute(lax.slice_in_dim(block, 0, width, axis=dim), axis, backward)
        block = jnp.concatenate([low, block, high], axis=dim)
    return block


def gelu_tanh(values):
    inner = COEF * (values + CUBIC * values * values * values)
    return 0.5 * values * (1.0 + jnp.tanh(inner))


def gelu_slope(values):
    tangent = jnp.tanh(COEF * (values + CUBIC * values * values * values))
    return 0.5 * (1.0 + tangent) + 0.5 * values * (1.0 - tangent * tangent) * COEF * (
        1.0 + 3.0 * CUBIC * values * values
    )


def depthwise(padded, taps):
    height = padded.shape[1] - 6
    width = padded.shape[2] - 6
    total = jnp.zeros((padded.shape[0], height, width, padded.shape[3]), jnp.float32)
    for row_tap in range(7):
        for col_tap in range(7):
            window = padded[:, row_tap : row_tap + height, col_tap : col_tap + width, :].astype(
                jnp.float32
            )
            total = total + window * taps[row_tap, col_tap]
    return total


def tap_grads(padded, upstream):
    height = upstream.shape[1]
    width = upstream.shape[2]
    rows_out = []
    for row_tap in range(7):
        line = []
        for col_tap in range(7):
            window = padded[:, row_tap : row_tap + height, col_tap : col_tap + width, :].astype(
                jnp.float32
            )
            line.append(jnp.sum(window * upstream, axis=(0, 1, 2)))
        rows_out.append(jnp.stack(line))
    return jnp.stack(rows_out)


def forward_layer(
    padded, current, taps, tap_bias, gain, shift, weight_in, bias_in, weight_out, bias_out, scale
):
    channels = current.shape[-1]
    mixed = (depthwise(padded, taps) + tap_bias).reshape(-1, channels)
    center = mixed - jnp.mean(mixed, -1, keepdims=True)
    rstd = lax.rsqrt(jnp.mean(center * center, -1, keepdims=True) + EPSILON)
    normed = center * rstd
    normal_low = (normed * gain + shift).astype(jnp.bfloat16)
    hidden = jnp.dot(normal_low, weight_in, preferred_element_type=jnp.float32) + bias_in
    activated = gelu_tanh(hidden).astype(jnp.bfloat16)
    branch = jnp.dot(activated, weight_out, preferred_element_type=jnp.float32) + bias_out
    result = current.reshape(-1, channels).astype(jnp.float32) + scale * branch
    result = result.astype(jnp.bfloat16).reshape(current.shape)
    return (result, (normed, rstd, normal_low, hidden, activated, branch))


def backward_layer(upstream, saved, gain, weight_in, weight_out, scale):
    normed, rstd, normal_low, hidden, activated, branch = saved
    contract_rows = (((0,), (0,)), ((), ()))
    contract_cols = (((1,), (1,)), ((), ()))
    grad_scale = jnp.sum(upstream * branch, 0)
    grad_branch = upstream * scale
    grad_bias_out = jnp.sum(grad_branch, 0)
    branch_low = grad_branch.astype(jnp.bfloat16)
    grad_weight_out = lax.dot_general(
        branch_low, activated, contract_rows, preferred_element_type=jnp.float32
    )
    grad_act = lax.dot_general(
        branch_low, weight_out, contract_cols, preferred_element_type=jnp.float32
    )
    grad_hidden = grad_act * gelu_slope(hidden)
    grad_bias_in = jnp.sum(grad_hidden, 0)
    hidden_low = grad_hidden.astype(jnp.bfloat16)
    grad_weight_in = lax.dot_general(
        normal_low, hidden_low, contract_rows, preferred_element_type=jnp.float32
    )
    grad_normal = lax.dot_general(
        hidden_low, weight_in, contract_cols, preferred_element_type=jnp.float32
    )
    grad_gain = jnp.sum(grad_normal * normed, 0)
    grad_shift = jnp.sum(grad_normal, 0)
    scaled = grad_normal * gain
    grad_mixed = rstd * (
        scaled
        - jnp.mean(scaled, -1, keepdims=True)
        - normed * jnp.mean(scaled * normed, -1, keepdims=True)
    )
    grad_tap_bias = jnp.sum(grad_mixed, 0)
    channel_grads = jnp.stack([grad_tap_bias, grad_gain, grad_shift, grad_bias_out, grad_scale])
    return (grad_mixed, grad_weight_in, grad_weight_out, grad_bias_in, channel_grads)


def reduce_weights(grad_in, grad_out):
    core = lax.axis_index("core")
    both = jnp.stack([grad_in, grad_out], 1).astype(jnp.bfloat16)
    keep = lax.dynamic_slice_in_dim(both, core * HALF, HALF, 2)
    give = lax.dynamic_slice_in_dim(both, (1 - core) * HALF, HALF, 2)
    pair = keep.astype(jnp.float32) + swapped(give, "core").astype(jnp.float32)
    pair = pair.astype(jnp.bfloat16).reshape(64, 8, 2, HALF)
    pieces = lax.all_to_all(pair, ("dp", *SPACE), 0, 0, tiled=True)
    mine = jnp.sum(pieces.astype(jnp.float32), 0).astype(jnp.bfloat16)
    copies = jnp.broadcast_to(mine, (32, *mine.shape))
    whole = lax.all_to_all(copies, SPACE, 0, 0, tiled=True).reshape(256, 2, HALF)
    mate = swapped(whole, "core")
    first = core == 0
    full = jnp.concatenate(
        [jnp.where(first, whole, mate), jnp.where(first, mate, whole)], 2
    ).astype(jnp.float32)
    return (full[:, 0], full[:, 1].T)


def reduce_small(parts):
    axes = ("xh", "y", "core", "z", "dp")
    lines = jnp.concatenate([p.reshape(-1) for p in parts])
    count = lines.shape[0]
    spare = -count % (128 * 128)
    lines = jnp.pad(lines, (0, spare)).astype(jnp.bfloat16).reshape(128, -1)
    pieces = lax.all_to_all(lines, axes, 0, 0, tiled=True)
    mine = jnp.sum(pieces.astype(jnp.float32), 0, keepdims=True)
    whole = lax.all_gather(mine, axes, axis=0, tiled=True).reshape(-1)
    outs = []
    start = 0
    for p in parts:
        outs.append(whole[start : start + p.size].reshape(p.shape))
        start += p.size
    return outs


def per_device(
    slides,
    cotangent,
    kernel,
    kernel_bias,
    norm_gain,
    norm_bias,
    weight_in,
    bias_in,
    weight_out,
    bias_out,
    layer_scale,
):
    layers = weight_in.shape[0]
    channels = slides.shape[-1]
    current = slides
    caches = []
    paddings = []
    fetched = []
    for which in range(layers):
        full_in, full_out = fetch_weights(weight_in[which], weight_out[which])
        fetched.append((full_in, full_out))
        padded = with_halo(current, ((("xh", "y", "core"), 1), ("z", 2)), 3)
        current, cache = forward_layer(
            padded,
            current,
            kernel[which],
            kernel_bias[which],
            norm_gain[which],
            norm_bias[which],
            full_in,
            bias_in[which],
            full_out,
            bias_out[which],
            layer_scale[which],
        )
        caches.append(cache)
        paddings.append(padded)
    upstream = cotangent.astype(jnp.float32).reshape(-1, channels)
    grads_in = [None] * layers
    grads_out = [None] * layers
    grads_kernel = [None] * layers
    grads_channel = [None] * layers
    grads_bias = [None] * layers
    for which in reversed(range(layers)):
        full_in, full_out = fetched[which]
        grad_mixed, grad_in, grad_out, grad_bias, channel_grads = backward_layer(
            upstream, caches[which], norm_gain[which], full_in, full_out, layer_scale[which]
        )
        shaped = grad_mixed.reshape(slides.shape)
        rim = with_halo(
            shaped.astype(jnp.bfloat16), ((("xh", "y", "core"), 1), ("z", 2)), 3
        ).astype(shaped.dtype)
        local_taps = tap_grads(paddings[which], shaped)
        back = depthwise(rim, kernel[which][::-1, ::-1])
        upstream = upstream + back.reshape(-1, channels)
        grads_in[which], grads_out[which] = reduce_weights(grad_in, grad_out)
        grads_kernel[which], grads_channel[which], grads_bias[which] = (
            local_taps,
            channel_grads,
            grad_bias,
        )
    grad_slides = upstream.astype(jnp.bfloat16).reshape(slides.shape)
    small = reduce_small([jnp.stack(grads_kernel), jnp.stack(grads_channel), jnp.stack(grads_bias)])
    return (current, grad_slides, jnp.stack(grads_in), jnp.stack(grads_out), *small)


def solution(mesh):
    fine = jax.sharding.Mesh(mesh.devices.reshape(2, 4, 2, 4, 2), ("xh", "y", "core", "z", "dp"))
    rows = ("xh", "y", "core")
    return jax.shard_map(
        per_device,
        mesh=fine,
        in_specs=(
            P("dp", rows, "z", None),
            P("dp", rows, "z", None),
            P(),
            P(),
            P(),
            P(),
            P(None, "dp", None),
            P(),
            P(None, None, "dp"),
            P(),
            P(),
        ),
        out_specs=(
            P("dp", rows, "z", None),
            P("dp", rows, "z", None),
            P(None, "dp", None),
            P(None, None, "dp"),
            P(),
            P(),
            P(),
        ),
        check_vma=False,
    )
```

profile of v0, /device:TPU:1, one launch (start us, length us, event | category | flops | bytes accessed | tf_op | source)
XLA Modules:
  0.0 720.8 jit_solution(1753578063245275340)
XLA Ops:
  11.6 4.3 collective-permute-start
  34.6 4.2 collective-permute-start.2
  41.0 15.6 %fusion.394 = (f32[16,32]{1,0:T(8,128)S(1)}, f32[1,16,32,512]{3,2,1,0:T(8,128)S(1)}) fusion(f32[512]{0:T(512)} %bitcast.599, f32[512]{0:T(512)S(1)} %bitcast.396, bf16[1,22,3,512]{3,2,1,0:T(4,128)(2,1)} %copy-done.36, bf16[1,22,32,512]{3,2,1,0:T(8,128)(2,1)S(1)} %get-tuple-element.321, f32[512]{0:T(512)S(1)} %bitcast.398, f32[512]{0:T(512)S(1)} %bitcast.400, ...), kind=kLoop, calls=%fused_computation.914 | loop fusion | flops 71826944 | bytes 5679104 | tf_op jit(solution)/shard_map/reduce_sum | solution.py:110
  95.5 11.4 %fusion.392 = (f32[16,32]{1,0:T(8,128)S(1)}, f32[1,16,32,512]{3,2,1,0:T(8,128)}) fusion(f32[512]{0:T(512)} %bitcast.604, f32[512]{0:T(512)S(1)} %bitcast.494, bf16[1,22,35,512]{3,2,1,0:T(8,128)(2,1)S(1)} %get-tuple-element.200, f32[512]{0:T(512)S(1)} %bitcast.497, f32[512]{0:T(512)S(1)} %bitcast.499, f32[512]{0:T(512)S(1)} %bitcast.501, ...), kind=kLoop, calls=%fused_computation.913 | loop fusion | flops 40369664 | bytes 23894016 | tf_op jit(solution)/shard_map/reduce_sum | solution.py:110
  113.1 4.2 fusion.416
  122.8 4.3 fusion.223
  133.1 5.6 collective-permute-start.16
  154.4 4.2 collective-permute-start.18
  184.8 10.3 %multiply_reduce_fusion.2 = (bf16[512]{0:T(512)(128)(2,1)}, bf16[512]{0:T(512)(128)(2,1)S(1)}, f32[1,16,32,512]{3,2,1,0:T(8,128)S(1)}) fusion(bf16[1,16,32,512]{3,2,1,0:T(8,128)(2,1)} %param.12, f32[512]{0:T(512)} %bitcast.601, f32[512]{0:T(512)} %bitcast.591, f32[512]{0:T(512)S(1)} %bitcast.493, f32[1,22,38,512]{3,2,1,0:T(8,128)S(1)} %maximum_convert_fusion.2, ...), kind=kLoop, calls=%fused_computation.716 | loop fusion | flops 26999808 | bytes 53059584 | tf_op jit(solution)/shard_map/reduce_sum | solution.py:128
  234.5 14.5 %all-to-all-start.4 = ((bf16[128,2,256]{2,1,0:T(2,128)(2,1)}), bf16[128,2,256]{2,1,0:T(2,128)(2,1)S(1)}, u32[]{:S(2)}, u32[]{:S(2)}) async-start(bf16[128,2,256]{2,1,0:T(2,128)(2,1)} %reshape.941), calls=%async_computation.4 | async-start | bytes 262144 | tf_op jit(solution)/shard_map/all_to_all | solution.py:183
  253.8 5.1 all-to-all-done.4
  258.9 5.7 all-to-all-start.2
  269.3 22.3 %all-to-all-done.2 = bf16[64,8,2,1024]{3,1,2,0:T(8,128)(2,1)} async-done(((bf16[64,8,2,1024]{3,1,2,0:T(8,128)(2,1)}), bf16[64,8,2,1024]{3,1,2,0:T(8,128)(2,1)}, u32[]{:S(2)}, u32[]{:S(2)}) %all-to-all-start.2) | async-done | bytes 2097184 | tf_op jit(solution)/shard_map/all_to_all | solution.py:165
  291.7 8.1 %all-to-all-start = ((bf16[64,8,2,1024]{3,1,2,0:T(8,128)(2,1)}), bf16[64,8,2,1024]{3,1,2,0:T(8,128)(2,1)}, u32[]{:S(2)}, u32[]{:S(2)}) async-start(bf16[64,8,2,1024]{3,1,2,0:T(8,128)(2,1)} %copy.26), calls=%async_computation | async-start | bytes 4194304 | tf_op jit(solution)/shard_map/all_to_all | solution.py:165
  301.7 23.7 %all-to-all-done = bf16[64,8,2,1024]{3,1,2,0:T(8,128)(2,1)} async-done(((bf16[64,8,2,1024]{3,1,2,0:T(8,128)(2,1)}), bf16[64,8,2,1024]{3,1,2,0:T(8,128)(2,1)}, u32[]{:S(2)}, u32[]{:S(2)}) %all-to-all-start) | async-done | bytes 2097184 | tf_op jit(solution)/shard_map/all_to_all | solution.py:165
  326.4 8.3 %all-to-all-start.3 = ((bf16[32,8,2,1024]{3,1,2,0:T(8,128)(2,1)}), bf16[32,8,2,1024]{3,1,2,0:T(8,128)(2,1)S(1)}, u32[]{:S(2)}, u32[]{:S(2)}) async-start(bf16[32,8,2,1024]{3,1,2,0:T(8,128)(2,1)} %broadcast_in_dim.7), calls=%async_computation.3 | async-start | bytes 2097152 | tf_op jit(solution)/shard_map/all_to_all | solution.py:168
  337.0 13.3 %all-to-all-done.3 = bf16[32,8,2,1024]{3,1,2,0:T(8,128)(2,1)S(1)} async-done(((bf16[32,8,2,1024]{3,1,2,0:T(8,128)(2,1)}), bf16[32,8,2,1024]{3,1,2,0:T(8,128)(2,1)S(1)}, u32[]{:S(2)}, u32[]{:S(2)}) %all-to-all-start.3) | async-done | bytes 1048608 | tf_op jit(solution)/shard_map/all_to_all | solution.py:168
  351.4 6.2 all-to-all-start.1
  357.6 4.2 collective-permute-start.21
  365.1 6.7 collective-permute-done.21
  377.6 293.8 %all-gather.1 = f32[128,1,512]{2,1,0:T(1,128)S(1)} all-gather(f32[1,1,512]{2,1,0:T(1,128)S(1)} %bitcast.600), channel_id=2, replica_groups=mesh['xh'=2,'y'=4,'core'=2,'z'=4,'dp'=2] {'xh','y','core','z','dp'}, dimensions={0}, use_global_device_ids=true | all-gather | bytes 264192 | tf_op jit(solution)/shard_map/all_gather | solution.py:185
  676.6 16.4 %collective-permute-start.27 = (bf16[256,2,1024]{2,0,1:T(8,128)(2,1)}, bf16[256,2,1024]{2,0,1:T(8,128)(2,1)}, u32[]{:S(2)}, u32[]{:S(2)}) collective-permute-start(bf16[256,2,1024]{2,0,1:T(8,128)(2,1)} %bitcast.371), channel_id=1, source_target_pairs={{0,8},{8,0},{1,9},{9,1},{2,10},{10,2},{3,11},{11,3},{4,12},{12,4},... | collective-permute-start | bytes 3145736 | tf_op jit(solution)/shard_map/ppermute | solution.py:23
  694.5 9.4 %fusion.226 = bf16[1,16,32,512]{3,2,1,0:T(8,128)(2,1)} fusion(f32[1,22,38,512]{3,2,1,0:T(8,128)S(1)} %maximum_convert_fusion.3, f32[1,16,32,512]{3,2,1,0:T(8,128)} %copy-done.23, bf16[1,16,32,512]{3,2,1,0:T(8,128)(2,1)} %param.12, f32[512]{0:T(512)S(1)} %bitcast.397, f32[512]{0:T(512)S(1)} %bitcast.399, f32[512]{0:T(512)S(1)} %bitcast.401, ...), kind=kLoop, calls=%fused_computation.493 | loop fusion | flops 26476544 | bytes 53577728 | tf_op jit(solution)/shard_map/convert_element_type | solution.py:256
  711.3 5.3 copy.31
  (525 shorter events, 210.5 us)
Async XLA Ops:
  5.4 56.6 %collective-permute-start.14 = (bf16[1024,256]{1,0:T(8,128)(2,1)}, bf16[1024,256]{1,0:T(8,128)(2,1)}, u32[]{:S(2)}, u32[]{:S(2)}) collective-permute-start(bf16[1024,256]{1,0:T(8,128)(2,1)} %dynamic-slice_bitcast_fusion), channel_id=1, source_target_pairs={{0,65},{1,0},{64,1},{65,64},{2,67},{3,2},{66,3},{67,66},{4,69},{5,... | collective-permute-start | bytes 1572872 | tf_op jit(solution)/shard_map/ppermute | solution.py:32
  9.5 53.0 %collective-permute-start.6 = (bf16[1024,256]{1,0:T(8,128)(2,1)}, bf16[1024,256]{1,0:T(8,128)(2,1)}, u32[]{:S(2)}, u32[]{:S(2)}) collective-permute-start(bf16[1024,256]{1,0:T(8,128)(2,1)} %dynamic-slice_bitcast_fusion.2), channel_id=1, source_target_pairs={{0,65},{1,0},{64,1},{65,64},{2,67},{3,2},{66,3},{67,66},{4,69},{5,... | collective-permute-start | bytes 1572872 | tf_op jit(solution)/shard_map/ppermute | solution.py:32
  11.6 19.3 %collective-permute-start = (bf16[1,3,32,512]{3,2,1,0:T(8,128)(2,1)S(1)}, bf16[1,3,32,512]{3,2,1,0:T(8,128)(2,1)S(1)}, u32[]{:S(2)}, u32[]{:S(2)}) collective-permute-start(bf16[1,3,32,512]{3,2,1,0:T(8,128)(2,1)S(1)} %get-tuple-element.217), channel_id=1, source_target_pairs={{0,8},{8,16},{16,24},{24,32},{32,40},{40,48},{48,56},{56,64},{64,7... | collective-permute-start | bytes 294920 | tf_op jit(solution)/shard_map/ppermute | solution.py:57
  16.0 16.2 %collective-permute-start.1 = (bf16[1,3,32,512]{3,2,1,0:T(8,128)(2,1)}, bf16[1,3,32,512]{3,2,1,0:T(8,128)(2,1)}, u32[]{:S(2)}, u32[]{:S(2)}) collective-permute-start(bf16[1,3,32,512]{3,2,1,0:T(8,128)(2,1)} %get-tuple-element.216), channel_id=1, source_target_pairs={{8,0},{16,8},{24,16},{32,24},{40,32},{48,40},{56,48},{64,56},{72,6... | collective-permute-start | bytes 294920 | tf_op jit(solution)/shard_map/ppermute | solution.py:60
  21.3 35.3 %collective-permute-start.12 = (bf16[128,2048]{1,0:T(8,128)(2,1)}, bf16[128,2048]{1,0:T(8,128)(2,1)}, u32[]{:S(2)}, u32[]{:S(2)}) collective-permute-start(bf16[128,2048]{1,0:T(8,128)(2,1)} %dynamic-slice_bitcast_fusion.1), channel_id=1, source_target_pairs={{0,1},{1,64},{64,65},{65,0},{2,3},{3,66},{66,67},{67,2},{4,5},{5,6... | collective-permute-start | bytes 1572872 | tf_op jit(solution)/shard_map/ppermute | solution.py:31
  39.4 21.4 %collective-permute-start.4 = (bf16[128,2048]{1,0:T(8,128)(2,1)}, bf16[128,2048]{1,0:T(8,128)(2,1)}, u32[]{:S(2)}, u32[]{:S(2)}) collective-permute-start(bf16[128,2048]{1,0:T(8,128)(2,1)} %dynamic-slice_bitcast_fusion.3), channel_id=1, source_target_pairs={{0,1},{1,64},{64,65},{65,0},{2,3},{3,66},{66,67},{67,2},{4,5},{5,6... | collective-permute-start | bytes 1572872 | tf_op jit(solution)/shard_map/ppermute | solution.py:31
  62.5 8.2 %collective-permute-start.7 = (bf16[1024,256]{1,0:T(8,128)(2,1)}, bf16[1024,256]{1,0:T(8,128)(2,1)S(1)}, u32[]{:S(2)}, u32[]{:S(2)}) collective-permute-start(bf16[1024,256]{1,0:T(8,128)(2,1)} %collective-permute-done.6), channel_id=1, source_target_pairs={{0,8},{8,0},{1,9},{9,1},{2,10},{10,2},{3,11},{11,3},{4,12},{12,4},... | collective-permute-start | bytes 1572872 | tf_op jit(solution)/shard_map/ppermute | solution.py:23
  131.2 20.8 %collective-permute-start.17 = (bf16[1,3,32,512]{3,2,1,0:T(8,128)(2,1)}, bf16[1,3,32,512]{3,2,1,0:T(8,128)(2,1)S(1)}, u32[]{:S(2)}, u32[]{:S(2)}) collective-permute-start(bf16[1,3,32,512]{3,2,1,0:T(8,128)(2,1)} %get-tuple-element.210), channel_id=1, source_target_pairs={{8,0},{16,8},{24,16},{32,24},{40,32},{48,40},{56,48},{64,56},{72,6... | collective-permute-start | bytes 294920 | tf_op jit(solution)/shard_map/ppermute | solution.py:60
  133.1 18.9 %collective-permute-start.16 = (bf16[1,3,32,512]{3,2,1,0:T(8,128)(2,1)}, bf16[1,3,32,512]{3,2,1,0:T(8,128)(2,1)S(1)}, u32[]{:S(2)}, u32[]{:S(2)}) collective-permute-start(bf16[1,3,32,512]{3,2,1,0:T(8,128)(2,1)} %get-tuple-element.209), channel_id=1, source_target_pairs={{0,8},{8,16},{16,24},{24,32},{32,40},{40,48},{48,56},{56,64},{64,7... | collective-permute-start | bytes 294920 | tf_op jit(solution)/shard_map/ppermute | solution.py:57
  140.3 108.7 %collective-permute-start.26 = (bf16[512,2,1024]{2,0,1:T(8,128)(2,1)}, bf16[512,2,1024]{2,0,1:T(8,128)(2,1)}, u32[]{:S(2)}, u32[]{:S(2)}) collective-permute-start(bf16[512,2,1024]{2,0,1:T(8,128)(2,1)} %fusion.18), channel_id=1, source_target_pairs={{0,8},{8,0},{1,9},{9,1},{2,10},{10,2},{3,11},{11,3},{4,12},{12,4},... | collective-permute-start | bytes 6291464 | tf_op jit(solution)/shard_map/ppermute | solution.py:23
  153.1 30.2 %collective-permute-start.19 = (bf16[1,22,3,512]{3,2,1,0:T(4,128)(2,1)S(1)}, bf16[1,22,3,512]{3,2,1,0:T(4,128)(2,1)S(1)}, u32[]{:S(2)}, u32[]{:S(2)}) collective-permute-start(bf16[1,22,3,512]{3,2,1,0:T(4,128)(2,1)S(1)} %get-tuple-element.198), channel_id=1, source_target_pairs={{2,0},{4,2},{6,4},{3,1},{5,3},{7,5},{10,8},{12,10},{14,12},{11,9},... | collective-permute-start | bytes 202760 | tf_op jit(solution)/shard_map/ppermute | solution.py:60
  154.4 28.9 %collective-permute-start.18 = (bf16[1,22,3,512]{3,2,1,0:T(4,128)(2,1)S(1)}, bf16[1,22,3,512]{3,2,1,0:T(4,128)(2,1)S(1)}, u32[]{:S(2)}, u32[]{:S(2)}) collective-permute-start(bf16[1,22,3,512]{3,2,1,0:T(4,128)(2,1)S(1)} %get-tuple-element.197), channel_id=1, source_target_pairs={{0,2},{2,4},{4,6},{1,3},{3,5},{5,7},{8,10},{10,12},{12,14},{9,11},... | collective-permute-start | bytes 202760 | tf_op jit(solution)/shard_map/ppermute | solution.py:57
  209.6 55.0 %collective-permute-start.24 = (bf16[512,2,1024]{2,0,1:T(8,128)(2,1)}, bf16[512,2,1024]{2,0,1:T(8,128)(2,1)}, u32[]{:S(2)}, u32[]{:S(2)}) collective-permute-start(bf16[512,2,1024]{2,0,1:T(8,128)(2,1)} %fusion.20), channel_id=1, source_target_pairs={{0,8},{8,0},{1,9},{9,1},{2,10},{10,2},{3,11},{11,3},{4,12},{12,4},... | collective-permute-start | bytes 6291464 | tf_op jit(solution)/shard_map/ppermute | solution.py:23
  234.5 24.4 %all-to-all-start.4 = ((bf16[128,2,256]{2,1,0:T(2,128)(2,1)}), bf16[128,2,256]{2,1,0:T(2,128)(2,1)S(1)}, u32[]{:S(2)}, u32[]{:S(2)}) async-start(bf16[128,2,256]{2,1,0:T(2,128)(2,1)} %reshape.941), calls=%async_computation.4 | async-start | bytes 262144 | tf_op jit(solution)/shard_map/all_to_all | solution.py:183
  258.9 32.8 %all-to-all-start.2 = ((bf16[64,8,2,1024]{3,1,2,0:T(8,128)(2,1)}), bf16[64,8,2,1024]{3,1,2,0:T(8,128)(2,1)}, u32[]{:S(2)}, u32[]{:S(2)}) async-start(bf16[64,8,2,1024]{3,1,2,0:T(8,128)(2,1)} %copy.28), calls=%async_computation.2 | async-start | bytes 4194304 | tf_op jit(solution)/shard_map/all_to_all | solution.py:165
  291.7 33.7 %all-to-all-start = ((bf16[64,8,2,1024]{3,1,2,0:T(8,128)(2,1)}), bf16[64,8,2,1024]{3,1,2,0:T(8,128)(2,1)}, u32[]{:S(2)}, u32[]{:S(2)}) async-start(bf16[64,8,2,1024]{3,1,2,0:T(8,128)(2,1)} %copy.26), calls=%async_computation | async-start | bytes 4194304 | tf_op jit(solution)/shard_map/all_to_all | solution.py:165
  326.4 23.8 %all-to-all-start.3 = ((bf16[32,8,2,1024]{3,1,2,0:T(8,128)(2,1)}), bf16[32,8,2,1024]{3,1,2,0:T(8,128)(2,1)S(1)}, u32[]{:S(2)}, u32[]{:S(2)}) async-start(bf16[32,8,2,1024]{3,1,2,0:T(8,128)(2,1)} %broadcast_in_dim.7), calls=%async_computation.3 | async-start | bytes 2097152 | tf_op jit(solution)/shard_map/all_to_all | solution.py:168
  351.4 341.6 %all-to-all-start.1 = ((bf16[32,8,2,1024]{3,1,2,0:T(8,128)(2,1)}), bf16[32,8,2,1024]{3,1,2,0:T(8,128)(2,1)}, u32[]{:S(2)}, u32[]{:S(2)}) async-start(bf16[32,8,2,1024]{3,1,2,0:T(8,128)(2,1)} %broadcast_in_dim.6), calls=%async_computation.1 | async-start | bytes 2097152 | tf_op jit(solution)/shard_map/all_to_all | solution.py:168
  357.6 14.2 %collective-permute-start.21 = (bf16[1,3,32,512]{3,2,1,0:T(8,128)(2,1)S(1)}, bf16[1,3,32,512]{3,2,1,0:T(8,128)(2,1)S(1)}, u32[]{:S(2)}, u32[]{:S(2)}) collective-permute-start(bf16[1,3,32,512]{3,2,1,0:T(8,128)(2,1)S(1)} %get-tuple-element.208), channel_id=1, source_target_pairs={{8,0},{16,8},{24,16},{32,24},{40,32},{48,40},{56,48},{64,56},{72,6... | collective-permute-start | bytes 294920 | tf_op jit(solution)/shard_map/ppermute | solution.py:60
  361.8 10.0 %collective-permute-start.20 = (bf16[1,3,32,512]{3,2,1,0:T(8,128)(2,1)S(1)}, bf16[1,3,32,512]{3,2,1,0:T(8,128)(2,1)S(1)}, u32[]{:S(2)}, u32[]{:S(2)}) collective-permute-start(bf16[1,3,32,512]{3,2,1,0:T(8,128)(2,1)S(1)} %get-tuple-element.207), channel_id=1, source_target_pairs={{0,8},{8,16},{16,24},{24,32},{32,40},{40,48},{48,56},{56,64},{64,7... | collective-permute-start | bytes 294920 | tf_op jit(solution)/shard_map/ppermute | solution.py:57
  371.9 302.3 %collective-permute-start.23 = (bf16[1,22,3,512]{3,2,1,0:T(4,128)(2,1)S(1)}, bf16[1,22,3,512]{3,2,1,0:T(4,128)(2,1)S(1)}, u32[]{:S(2)}, u32[]{:S(2)}) collective-permute-start(bf16[1,22,3,512]{3,2,1,0:T(4,128)(2,1)S(1)} %get-tuple-element.196), channel_id=1, source_target_pairs={{2,0},{4,2},{6,4},{3,1},{5,3},{7,5},{10,8},{12,10},{14,12},{11,9},... | collective-permute-start | bytes 202760 | tf_op jit(solution)/shard_map/ppermute | solution.py:60
  373.2 301.0 %collective-permute-start.22 = (bf16[1,22,3,512]{3,2,1,0:T(4,128)(2,1)S(1)}, bf16[1,22,3,512]{3,2,1,0:T(4,128)(2,1)S(1)}, u32[]{:S(2)}, u32[]{:S(2)}) collective-permute-start(bf16[1,22,3,512]{3,2,1,0:T(4,128)(2,1)S(1)} %get-tuple-element.195), channel_id=1, source_target_pairs={{0,2},{2,4},{4,6},{1,3},{3,5},{5,7},{8,10},{10,12},{12,14},{9,11},... | collective-permute-start | bytes 202760 | tf_op jit(solution)/shard_map/ppermute | solution.py:57
  676.6 27.3 %collective-permute-start.27 = (bf16[256,2,1024]{2,0,1:T(8,128)(2,1)}, bf16[256,2,1024]{2,0,1:T(8,128)(2,1)}, u32[]{:S(2)}, u32[]{:S(2)}) collective-permute-start(bf16[256,2,1024]{2,0,1:T(8,128)(2,1)} %bitcast.371), channel_id=1, source_target_pairs={{0,8},{8,0},{1,9},{9,1},{2,10},{10,2},{3,11},{11,3},{4,12},{12,4},... | collective-permute-start | bytes 3145736 | tf_op jit(solution)/shard_map/ppermute | solution.py:23
  694.3 9.6 %collective-permute-start.25 = (bf16[256,2,1024]{2,0,1:T(8,128)(2,1)S(1)}, bf16[256,2,1024]{2,0,1:T(8,128)(2,1)S(1)}, u32[]{:S(2)}, u32[]{:S(2)}) collective-permute-start(bf16[256,2,1024]{2,0,1:T(8,128)(2,1)S(1)} %bitcast.382), channel_id=1, source_target_pairs={{0,8},{8,0},{1,9},{9,1},{2,10},{10,2},{3,11},{11,3},{4,12},{12,4},... | collective-permute-start | bytes 3145736 | tf_op jit(solution)/shard_map/ppermute | solution.py:23
  (117 other events, 1654.6 us)
where the time goes:
time: 729 us; the launch traced here: 721 us
  blocking collectives  294 us (40%)
  starting transfers between devices  117 us (16%)
  other arithmetic  116 us (16%)
  local copies, waits for them, and re-layouts  85.3 us (12%)
  waiting for transfers between devices  76 us (10%)
  matrix products  28.8 us (4%)
    all_gather x1, blocking collectives, reduce_small(): whole = lax.all_gather(mine, axes, axis=0, tiled=True).reshape(-1)  294 us
    all_to_all x2, waiting for transfers between devices, reduce_weights(): pieces = lax.all_to_all(pair, ('dp', *SPACE), 0, 0, tiled=True)  46 us
    ppermute x8, starting transfers between devices, with_halo(): lax.ppermute(lax.slice_in_dim(block, block.shape[dim] - width, None, axis...  32.4 us
    another operation x112, local copies, waits for them, and re-layouts, tap_grads(): rows_out.append(jnp.stack(line))  32.1 us
    reduce_sum x2, other arithmetic, forward_layer(): center = mixed - jnp.mean(mixed, -1, keepdims=True)  27 us
    reduce_sum x9, other arithmetic, tap_grads(): line.append(jnp.sum(window * upstream, axis=(0, 1, 2)))  23.6 us
    ppermute x8, starting transfers between devices, swapped(): return lax.ppermute(value, axis, [(0, 1), (1, 0)])  21.5 us
    ppermute x8, starting transfers between devices, with_halo(): lax.ppermute(lax.slice_in_dim(block, 0, width, axis=dim), axis, backward)  16 us
  transfers between devices with their start and end apart: 33, of which 8 were waited for; matrix products, arithmetic and copies ran while one was open for 22% of the time, Pallas kernels for 0%

commit v1 on v0

--- a/solution.py
+++ b/solution.py
@@ -8,6 +8,11 @@
 EPSILON = 1e-06
 SPACE = ("xh", "y", "z")
 HALF = 1024
+
+
+def swapped_in(shard, axis, along):
+    sent = jnp.stack([shard] * lax.axis_size(axis))
+    return jnp.concatenate(lax.all_to_all(sent, axis, 0, 0), axis=along)
 
 
 def chips_along_x(step):
@@ -182,7 +187,7 @@
     lines = jnp.pad(lines, (0, spare)).astype(jnp.bfloat16).reshape(128, -1)
     pieces = lax.all_to_all(lines, axes, 0, 0, tiled=True)
     mine = jnp.sum(pieces.astype(jnp.float32), 0, keepdims=True)
-    whole = lax.all_gather(mine, axes, axis=0, tiled=True).reshape(-1)
+    whole = swapped_in(mine, axes, 0).reshape(-1)
     outs = []
     start = 0
     for p in parts:

time: 729 us -> 436 us (0.60)
  blocking collectives: 294 us -> 0 us
    all_gather x1 -> x0, blocking collectives: 294 us -> none  [reduce_small(): whole = lax.all_gather(mine, axes, axis=0, tiled=True).reshape(-1)]
    ppermute x8, starting transfers between devices: 21.5 us -> 6.04 us  [swapped(): return lax.ppermute(value, axis, [(0, 1), (1, 0)])]
    all_to_all x0 -> x1, starting transfers between devices: none -> 10.5 us  [swapped_in(): return jnp.concatenate(lax.all_to_all(sent, axis, 0, 0), axis=along)]
  transfers between devices with their start and end apart: 33 -> 34, of which waited for: 8 -> 8; matrix products, arithmetic and copies ran while one was open for 22% -> 39% of each run, Pallas kernels for 0% -> 0%
where the time goes in v1:
time: 436 us; the launch traced here: 427 us
  other arithmetic  117 us (27%)
  starting transfers between devices  112 us (26%)
  local copies, waits for them, and re-layouts  89.8 us (21%)
  waiting for transfers between devices  76.3 us (18%)
  matrix products  28.7 us (7%)
    all_to_all x2, waiting for transfers between devices, reduce_weights(): pieces = lax.all_to_all(pair, ('dp', *SPACE), 0, 0, tiled=True)  46 us
    ppermute x8, starting transfers between devices, with_halo(): lax.ppermute(lax.slice_in_dim(block, block.shape[dim] - width, None, axis...  33 us
    another operation x112, local copies, waits for them, and re-layouts, tap_grads(): rows_out.append(jnp.stack(line))  32.1 us
    reduce_sum x2, other arithmetic, forward_layer(): center = mixed - jnp.mean(mixed, -1, keepdims=True)  27 us
    reduce_sum x9, other arithmetic, tap_grads(): line.append(jnp.sum(window * upstream, axis=(0, 1, 2)))  23.6 us
    ppermute x8, starting transfers between devices, with_halo(): lax.ppermute(lax.slice_in_dim(block, 0, width, axis=dim), axis, backward)  16 us
    all_to_all x2, starting transfers between devices, reduce_weights(): lax.all_to_all(copies, SPACE, 0, 0, tiled=True).reshape(256, 2, HALF)  14.5 us
    all_to_all x2, starting transfers between devices, reduce_weights(): pieces = lax.all_to_all(pair, ('dp', *SPACE), 0, 0, tiled=True)  13.8 us
  transfers between devices with their start and end apart: 34, of which 8 were waited for; matrix products, arithmetic and copies ran while one was open for 39% of the time, Pallas kernels for 0%

profile of v1, /device:TPU:1, one launch (start us, length us, event | category | flops | bytes accessed | tf_op | source)
XLA Modules:
  0.0 427.2 jit_solution(4317246651315442265)
XLA Ops:
  12.2 4.3 %collective-permute-start = (bf16[1,3,32,512]{3,2,1,0:T(8,128)(2,1)}, bf16[1,3,32,512]{3,2,1,0:T(8,128)(2,1)}, u32[]{:S(2)}, u32[]{:S(2)}) collective-permute-start(bf16[1,3,32,512]{3,2,1,0:T(8,128)(2,1)} %get-tuple-element.217), channel_id=1, source_target_pairs={{0,8},{8,16},{16,24},{24,32},{32,40},{40,48},{48,56},{56,64},{64,7... | collective-permute-start | bytes 294920 | tf_op jit(solution)/shard_map/ppermute | solution.py:62
  36.0 4.2 collective-permute-start.2
  42.4 15.6 %fusion.394 = (f32[16,32]{1,0:T(8,128)S(1)}, f32[1,16,32,512]{3,2,1,0:T(8,128)S(1)}) fusion(f32[512]{0:T(512)} %bitcast.597, f32[512]{0:T(512)S(1)} %bitcast.394, bf16[1,22,3,512]{3,2,1,0:T(4,128)(2,1)} %copy-done.35, bf16[1,22,32,512]{3,2,1,0:T(8,128)(2,1)S(1)} %get-tuple-element.321, f32[512]{0:T(512)S(1)} %bitcast.396, f32[512]{0:T(512)S(1)} %bitcast.398, ...), kind=kLoop, calls=%fused_computation.914 | loop fusion | flops 71826944 | bytes 5679104 | tf_op jit(solution)/shard_map/reduce_sum | solution.py:115
  96.7 11.4 %fusion.392 = (f32[16,32]{1,0:T(8,128)S(1)}, f32[1,16,32,512]{3,2,1,0:T(8,128)}) fusion(f32[512]{0:T(512)} %bitcast.601, f32[512]{0:T(512)S(1)} %bitcast.492, bf16[1,22,35,512]{3,2,1,0:T(8,128)(2,1)S(1)} %get-tuple-element.200, f32[512]{0:T(512)S(1)} %bitcast.495, f32[512]{0:T(512)S(1)} %bitcast.497, f32[512]{0:T(512)S(1)} %bitcast.499, ...), kind=kLoop, calls=%fused_computation.913 | loop fusion | flops 40369664 | bytes 23894016 | tf_op jit(solution)/shard_map/reduce_sum | solution.py:115
  114.3 4.2 fusion.416
  124.0 4.3 %fusion.223 = (bf16[512]{0:T(512)(128)(2,1)S(1)}, bf16[512]{0:T(512)(128)(2,1)S(1)}, bf16[512]{0:T(512)(128)(2,1)}, bf16[512]{0:T(512)(128)(2,1)}, bf16[512]{0:T...) fusion(bf16[1,22,35,512]{3,2,1,0:T(8,128)(2,1)S(1)} %get-tuple-, ...), kind=kLoop, calls=%fused_computation.489 | loop fusion | flops 15981568 | bytes 12611584 | tf_op jit(solution)/shard_map/reduce_sum | solution.py:105
  134.3 5.6 %collective-permute-start.16 = (bf16[1,3,32,512]{3,2,1,0:T(8,128)(2,1)}, bf16[1,3,32,512]{3,2,1,0:T(8,128)(2,1)S(1)}, u32[]{:S(2)}, u32[]{:S(2)}) collective-permute-start(bf16[1,3,32,512]{3,2,1,0:T(8,128)(2,1)} %get-tuple-element.209), channel_id=1, source_target_pairs={{0,8},{8,16},{16,24},{24,32},{32,40},{40,48},{48,56},{56,64},{64,7... | collective-permute-start | bytes 294920 | tf_op jit(solution)/shard_map/ppermute | solution.py:62
  155.6 4.2 collective-permute-start.18
  186.0 10.3 %multiply_reduce_fusion.2 = (bf16[512]{0:T(512)(128)(2,1)}, bf16[512]{0:T(512)(128)(2,1)S(1)}, f32[1,16,32,512]{3,2,1,0:T(8,128)S(1)}) fusion(bf16[1,16,32,512]{3,2,1,0:T(8,128)(2,1)} %param.12, f32[512]{0:T(512)} %bitcast.598, f32[512]{0:T(512)} %bitcast.589, f32[512]{0:T(512)S(1)} %bitcast.491, f32[1,22,38,512]{3,2,1,0:T(8,128)S(1)} %maximum_convert_fusion.2, ...), kind=kLoop, calls=%fused_computation.716 | loop fusion | flops 26999808 | bytes 53059584 | tf_op jit(solution)/shard_map/reduce_sum | solution.py:133
  235.7 13.6 %all-to-all-start.4 = ((bf16[128,2,256]{2,1,0:T(2,128)(2,1)}), bf16[128,2,256]{2,1,0:T(2,128)(2,1)S(1)}, u32[]{:S(2)}, u32[]{:S(2)}) async-start(bf16[128,2,256]{2,1,0:T(2,128)(2,1)} %reshape.927), calls=%async_computation.4 | async-start | bytes 262144 | tf_op jit(solution)/shard_map/all_to_all | solution.py:188
  254.1 5.1 %all-to-all-done.4 = bf16[128,2,256]{2,1,0:T(2,128)(2,1)S(1)} async-done(((bf16[128,2,256]{2,1,0:T(2,128)(2,1)}), bf16[128,2,256]{2,1,0:T(2,128)(2,1)S(1)}, u32[]{:S(2)}, u32[]{:S(2)}) %all-to-all-start.4) | async-done | bytes 131104 | tf_op jit(solution)/shard_map/all_to_all | solution.py:188
  259.2 5.7 %all-to-all-start.2 = ((bf16[64,8,2,1024]{3,1,2,0:T(8,128)(2,1)}), bf16[64,8,2,1024]{3,1,2,0:T(8,128)(2,1)}, u32[]{:S(2)}, u32[]{:S(2)}) async-start(bf16[64,8,2,1024]{3,1,2,0:T(8,128)(2,1)} %copy.28), calls=%async_computation.2 | async-start | bytes 4194304 | tf_op jit(solution)/shard_map/all_to_all | solution.py:170
  269.6 22.3 %all-to-all-done.2 = bf16[64,8,2,1024]{3,1,2,0:T(8,128)(2,1)} async-done(((bf16[64,8,2,1024]{3,1,2,0:T(8,128)(2,1)}), bf16[64,8,2,1024]{3,1,2,0:T(8,128)(2,1)}, u32[]{:S(2)}, u32[]{:S(2)}) %all-to-all-start.2) | async-done | bytes 2097184 | tf_op jit(solution)/shard_map/all_to_all | solution.py:170
  292.0 8.1 %all-to-all-start = ((bf16[64,8,2,1024]{3,1,2,0:T(8,128)(2,1)}), bf16[64,8,2,1024]{3,1,2,0:T(8,128)(2,1)}, u32[]{:S(2)}, u32[]{:S(2)}) async-start(bf16[64,8,2,1024]{3,1,2,0:T(8,128)(2,1)} %copy.26), calls=%async_computation | async-start | bytes 4194304 | tf_op jit(solution)/shard_map/all_to_all | solution.py:170
  302.0 23.7 %all-to-all-done = bf16[64,8,2,1024]{3,1,2,0:T(8,128)(2,1)} async-done(((bf16[64,8,2,1024]{3,1,2,0:T(8,128)(2,1)}), bf16[64,8,2,1024]{3,1,2,0:T(8,128)(2,1)}, u32[]{:S(2)}, u32[]{:S(2)}) %all-to-all-start) | async-done | bytes 2097184 | tf_op jit(solution)/shard_map/all_to_all | solution.py:170
  326.8 8.3 %all-to-all-start.3 = ((bf16[32,8,2,1024]{3,1,2,0:T(8,128)(2,1)}), bf16[32,8,2,1024]{3,1,2,0:T(8,128)(2,1)S(1)}, u32[]{:S(2)}, u32[]{:S(2)}) async-start(bf16[32,8,2,1024]{3,1,2,0:T(8,128)(2,1)} %broadcast_in_dim.5), calls=%async_computation.3 | async-start | bytes 2097152 | tf_op jit(solution)/shard_map/all_to_all | solution.py:173
  337.0 13.6 %all-to-all-done.3 = bf16[32,8,2,1024]{3,1,2,0:T(8,128)(2,1)S(1)} async-done(((bf16[32,8,2,1024]{3,1,2,0:T(8,128)(2,1)}), bf16[32,8,2,1024]{3,1,2,0:T(8,128)(2,1)S(1)}, u32[]{:S(2)}, u32[]{:S(2)}) %all-to-all-start.3) | async-done | bytes 1048608 | tf_op jit(solution)/shard_map/all_to_all | solution.py:173
  351.7 6.2 %all-to-all-start.1 = ((bf16[32,8,2,1024]{3,1,2,0:T(8,128)(2,1)}), bf16[32,8,2,1024]{3,1,2,0:T(8,128)(2,1)}, u32[]{:S(2)}, u32[]{:S(2)}) async-start(bf16[32,8,2,1024]{3,1,2,0:T(8,128)(2,1)} %broadcast_in_dim.4), calls=%async_computation.1 | async-start | bytes 2097152 | tf_op jit(solution)/shard_map/all_to_all | solution.py:173
  358.0 4.2 collective-permute-start.21
  365.5 6.7 %collective-permute-done.21 = bf16[1,3,32,512]{3,2,1,0:T(8,128)(2,1)S(1)} collective-permute-done((bf16[1,3,32,512]{3,2,1,0:T(8,128)(2,1)S(1)}, bf16[1,3,32,512]{3,2,1,0:T(8,128)(2,1)S(1)}, u32[]{:S(2)}, u32[]{:S(2)}) %collective-permute-start.21) | collective-permute-done | bytes 98336 | tf_op jit(solution)/shard_map/ppermute | solution.py:65
  373.7 4.6 %collective-permute-start.22 = (bf16[1,22,3,512]{3,2,1,0:T(4,128)(2,1)S(1)}, bf16[1,22,3,512]{3,2,1,0:T(4,128)(2,1)}, u32[]{:S(2)}, u32[]{:S(2)}) collective-permute-start(bf16[1,22,3,512]{3,2,1,0:T(4,128)(2,1)S(1)} %get-tuple-element.195), channel_id=1, source_target_pairs={{0,2},{2,4},{4,6},{1,3},{3,5},{5,7},{8,10},{10,12},{12,14},{9,11},... | collective-permute-start | bytes 202760 | tf_op jit(solution)/shard_map/ppermute | solution.py:62
  383.9 10.5 %all-to-all-start.5 = ((f32[128,1,512]{2,1,0:T(1,128)}), f32[128,1,512]{2,1,0:T(1,128)S(1)}, u32[]{:S(2)}, u32[]{:S(2)}) async-start(f32[128,1,512]{2,1,0:T(1,128)} %stack.794), calls=%async_computation.5 | async-start | bytes 524288 | tf_op jit(solution)/shard_map/all_to_all | solution.py:15
  397.9 9.3 %fusion.226 = bf16[1,16,32,512]{3,2,1,0:T(8,128)(2,1)} fusion(f32[1,22,38,512]{3,2,1,0:T(8,128)S(1)} %maximum_convert_fusion.3, f32[1,16,32,512]{3,2,1,0:T(8,128)} %copy-done.22, bf16[1,16,32,512]{3,2,1,0:T(8,128)(2,1)} %param.12, f32[512]{0:T(512)S(1)} %bitcast.395, f32[512]{0:T(512)S(1)} %bitcast.397, f32[512]{0:T(512)S(1)} %bitcast.399, ...), kind=kLoop, calls=%fused_computation.493 | loop fusion | flops 26476544 | bytes 53577728 | tf_op jit(solution)/shard_map/convert_element_type | solution.py:261
  417.7 5.3 %copy.31 = f32[2,2048,256]{2,1,0:T(8,128)} copy(f32[2,2048,256]{1,2,0:T(8,128)} %pad_maximum_fusion.1) | data formatting | bytes 8388608
  (551 shorter events, 212.5 us)
Async XLA Ops:
  5.7 57.6 %collective-permute-start.14 = (bf16[1024,256]{1,0:T(8,128)(2,1)}, bf16[1024,256]{1,0:T(8,128)(2,1)}, u32[]{:S(2)}, u32[]{:S(2)}) collective-permute-start(bf16[1024,256]{1,0:T(8,128)(2,1)} %dynamic-slice_bitcast_fusion), channel_id=1, source_target_pairs={{0,65},{1,0},{64,1},{65,64},{2,67},{3,2},{66,3},{67,66},{4,69},{5,... | collective-permute-start | bytes 1572872 | tf_op jit(solution)/shard_map/ppermute | solution.py:37
  10.9 52.9 %collective-permute-start.6 = (bf16[1024,256]{1,0:T(8,128)(2,1)}, bf16[1024,256]{1,0:T(8,128)(2,1)}, u32[]{:S(2)}, u32[]{:S(2)}) collective-permute-start(bf16[1024,256]{1,0:T(8,128)(2,1)} %dynamic-slice_bitcast_fusion.2), channel_id=1, source_target_pairs={{0,65},{1,0},{64,1},{65,64},{2,67},{3,2},{66,3},{67,66},{4,69},{5,... | collective-permute-start | bytes 1572872 | tf_op jit(solution)/shard_map/ppermute | solution.py:37
  12.2 20.3 %collective-permute-start = (bf16[1,3,32,512]{3,2,1,0:T(8,128)(2,1)}, bf16[1,3,32,512]{3,2,1,0:T(8,128)(2,1)}, u32[]{:S(2)}, u32[]{:S(2)}) collective-permute-start(bf16[1,3,32,512]{3,2,1,0:T(8,128)(2,1)} %get-tuple-element.217), channel_id=1, source_target_pairs={{0,8},{8,16},{16,24},{24,32},{32,40},{40,48},{48,56},{56,64},{64,7... | collective-permute-start | bytes 294920 | tf_op jit(solution)/shard_map/ppermute | solution.py:62
  16.5 17.0 %collective-permute-start.1 = (bf16[1,3,32,512]{3,2,1,0:T(8,128)(2,1)}, bf16[1,3,32,512]{3,2,1,0:T(8,128)(2,1)}, u32[]{:S(2)}, u32[]{:S(2)}) collective-permute-start(bf16[1,3,32,512]{3,2,1,0:T(8,128)(2,1)} %get-tuple-element.216), channel_id=1, source_target_pairs={{8,0},{16,8},{24,16},{32,24},{40,32},{48,40},{56,48},{64,56},{72,6... | collective-permute-start | bytes 294920 | tf_op jit(solution)/shard_map/ppermute | solution.py:65
  21.8 36.2 %collective-permute-start.12 = (bf16[128,2048]{1,0:T(8,128)(2,1)}, bf16[128,2048]{1,0:T(8,128)(2,1)}, u32[]{:S(2)}, u32[]{:S(2)}) collective-permute-start(bf16[128,2048]{1,0:T(8,128)(2,1)} %dynamic-slice_bitcast_fusion.1), channel_id=1, source_target_pairs={{0,1},{1,64},{64,65},{65,0},{2,3},{3,66},{66,67},{67,2},{4,5},{5,6... | collective-permute-start | bytes 1572872 | tf_op jit(solution)/shard_map/ppermute | solution.py:36
  40.8 21.4 %collective-permute-start.4 = (bf16[128,2048]{1,0:T(8,128)(2,1)}, bf16[128,2048]{1,0:T(8,128)(2,1)}, u32[]{:S(2)}, u32[]{:S(2)}) collective-permute-start(bf16[128,2048]{1,0:T(8,128)(2,1)} %dynamic-slice_bitcast_fusion.3), channel_id=1, source_target_pairs={{0,1},{1,64},{64,65},{65,0},{2,3},{3,66},{66,67},{67,2},{4,5},{5,6... | collective-permute-start | bytes 1572872 | tf_op jit(solution)/shard_map/ppermute | solution.py:36
  63.8 8.1 %collective-permute-start.7 = (bf16[1024,256]{1,0:T(8,128)(2,1)}, bf16[1024,256]{1,0:T(8,128)(2,1)S(1)}, u32[]{:S(2)}, u32[]{:S(2)}) collective-permute-start(bf16[1024,256]{1,0:T(8,128)(2,1)} %collective-permute-done.6), channel_id=1, source_target_pairs={{0,8},{8,0},{1,9},{9,1},{2,10},{10,2},{3,11},{11,3},{4,12},{12,4},... | collective-permute-start | bytes 1572872 | tf_op jit(solution)/shard_map/ppermute | solution.py:28
  132.4 20.8 %collective-permute-start.17 = (bf16[1,3,32,512]{3,2,1,0:T(8,128)(2,1)}, bf16[1,3,32,512]{3,2,1,0:T(8,128)(2,1)S(1)}, u32[]{:S(2)}, u32[]{:S(2)}) collective-permute-start(bf16[1,3,32,512]{3,2,1,0:T(8,128)(2,1)} %get-tuple-element.210), channel_id=1, source_target_pairs={{8,0},{16,8},{24,16},{32,24},{40,32},{48,40},{56,48},{64,56},{72,6... | collective-permute-start | bytes 294920 | tf_op jit(solution)/shard_map/ppermute | solution.py:65
  134.3 18.9 %collective-permute-start.16 = (bf16[1,3,32,512]{3,2,1,0:T(8,128)(2,1)}, bf16[1,3,32,512]{3,2,1,0:T(8,128)(2,1)S(1)}, u32[]{:S(2)}, u32[]{:S(2)}) collective-permute-start(bf16[1,3,32,512]{3,2,1,0:T(8,128)(2,1)} %get-tuple-element.209), channel_id=1, source_target_pairs={{0,8},{8,16},{16,24},{24,32},{32,40},{40,48},{48,56},{56,64},{64,7... | collective-permute-start | bytes 294920 | tf_op jit(solution)/shard_map/ppermute | solution.py:62
  141.5 107.9 %collective-permute-start.26 = (bf16[512,2,1024]{2,0,1:T(8,128)(2,1)}, bf16[512,2,1024]{2,0,1:T(8,128)(2,1)}, u32[]{:S(2)}, u32[]{:S(2)}) collective-permute-start(bf16[512,2,1024]{2,0,1:T(8,128)(2,1)} %fusion.18), channel_id=1, source_target_pairs={{0,8},{8,0},{1,9},{9,1},{2,10},{10,2},{3,11},{11,3},{4,12},{12,4},... | collective-permute-start | bytes 6291464 | tf_op jit(solution)/shard_map/ppermute | solution.py:28
  154.3 30.3 %collective-permute-start.19 = (bf16[1,22,3,512]{3,2,1,0:T(4,128)(2,1)S(1)}, bf16[1,22,3,512]{3,2,1,0:T(4,128)(2,1)S(1)}, u32[]{:S(2)}, u32[]{:S(2)}) collective-permute-start(bf16[1,22,3,512]{3,2,1,0:T(4,128)(2,1)S(1)} %get-tuple-element.198), channel_id=1, source_target_pairs={{2,0},{4,2},{6,4},{3,1},{5,3},{7,5},{10,8},{12,10},{14,12},{11,9},... | collective-permute-start | bytes 202760 | tf_op jit(solution)/shard_map/ppermute | solution.py:65
  155.6 29.0 %collective-permute-start.18 = (bf16[1,22,3,512]{3,2,1,0:T(4,128)(2,1)S(1)}, bf16[1,22,3,512]{3,2,1,0:T(4,128)(2,1)S(1)}, u32[]{:S(2)}, u32[]{:S(2)}) collective-permute-start(bf16[1,22,3,512]{3,2,1,0:T(4,128)(2,1)S(1)} %get-tuple-element.197), channel_id=1, source_target_pairs={{0,2},{2,4},{4,6},{1,3},{3,5},{5,7},{8,10},{10,12},{12,14},{9,11},... | collective-permute-start | bytes 202760 | tf_op jit(solution)/shard_map/ppermute | solution.py:62
  210.8 54.1 %collective-permute-start.24 = (bf16[512,2,1024]{2,0,1:T(8,128)(2,1)}, bf16[512,2,1024]{2,0,1:T(8,128)(2,1)}, u32[]{:S(2)}, u32[]{:S(2)}) collective-permute-start(bf16[512,2,1024]{2,0,1:T(8,128)(2,1)} %fusion.20), channel_id=1, source_target_pairs={{0,8},{8,0},{1,9},{9,1},{2,10},{10,2},{3,11},{11,3},{4,12},{12,4},... | collective-permute-start | bytes 6291464 | tf_op jit(solution)/shard_map/ppermute | solution.py:28
  235.7 23.5 %all-to-all-start.4 = ((bf16[128,2,256]{2,1,0:T(2,128)(2,1)}), bf16[128,2,256]{2,1,0:T(2,128)(2,1)S(1)}, u32[]{:S(2)}, u32[]{:S(2)}) async-start(bf16[128,2,256]{2,1,0:T(2,128)(2,1)} %reshape.927), calls=%async_computation.4 | async-start | bytes 262144 | tf_op jit(solution)/shard_map/all_to_all | solution.py:188
  259.2 32.8 %all-to-all-start.2 = ((bf16[64,8,2,1024]{3,1,2,0:T(8,128)(2,1)}), bf16[64,8,2,1024]{3,1,2,0:T(8,128)(2,1)}, u32[]{:S(2)}, u32[]{:S(2)}) async-start(bf16[64,8,2,1024]{3,1,2,0:T(8,128)(2,1)} %copy.28), calls=%async_computation.2 | async-start | bytes 4194304 | tf_op jit(solution)/shard_map/all_to_all | solution.py:170
  292.0 33.7 %all-to-all-start = ((bf16[64,8,2,1024]{3,1,2,0:T(8,128)(2,1)}), bf16[64,8,2,1024]{3,1,2,0:T(8,128)(2,1)}, u32[]{:S(2)}, u32[]{:S(2)}) async-start(bf16[64,8,2,1024]{3,1,2,0:T(8,128)(2,1)} %copy.26), calls=%async_computation | async-start | bytes 4194304 | tf_op jit(solution)/shard_map/all_to_all | solution.py:170
  326.8 23.8 %all-to-all-start.3 = ((bf16[32,8,2,1024]{3,1,2,0:T(8,128)(2,1)}), bf16[32,8,2,1024]{3,1,2,0:T(8,128)(2,1)S(1)}, u32[]{:S(2)}, u32[]{:S(2)}) async-start(bf16[32,8,2,1024]{3,1,2,0:T(8,128)(2,1)} %broadcast_in_dim.5), calls=%async_computation.3 | async-start | bytes 2097152 | tf_op jit(solution)/shard_map/all_to_all | solution.py:173
  351.7 30.7 %all-to-all-start.1 = ((bf16[32,8,2,1024]{3,1,2,0:T(8,128)(2,1)}), bf16[32,8,2,1024]{3,1,2,0:T(8,128)(2,1)}, u32[]{:S(2)}, u32[]{:S(2)}) async-start(bf16[32,8,2,1024]{3,1,2,0:T(8,128)(2,1)} %broadcast_in_dim.4), calls=%async_computation.1 | async-start | bytes 2097152 | tf_op jit(solution)/shard_map/all_to_all | solution.py:173
  358.0 14.1 %collective-permute-start.21 = (bf16[1,3,32,512]{3,2,1,0:T(8,128)(2,1)S(1)}, bf16[1,3,32,512]{3,2,1,0:T(8,128)(2,1)S(1)}, u32[]{:S(2)}, u32[]{:S(2)}) collective-permute-start(bf16[1,3,32,512]{3,2,1,0:T(8,128)(2,1)S(1)} %get-tuple-element.208), channel_id=1, source_target_pairs={{8,0},{16,8},{24,16},{32,24},{40,32},{48,40},{56,48},{64,56},{72,6... | collective-permute-start | bytes 294920 | tf_op jit(solution)/shard_map/ppermute | solution.py:65
  362.2 9.9 %collective-permute-start.20 = (bf16[1,3,32,512]{3,2,1,0:T(8,128)(2,1)S(1)}, bf16[1,3,32,512]{3,2,1,0:T(8,128)(2,1)S(1)}, u32[]{:S(2)}, u32[]{:S(2)}) collective-permute-start(bf16[1,3,32,512]{3,2,1,0:T(8,128)(2,1)S(1)} %get-tuple-element.207), channel_id=1, source_target_pairs={{0,8},{8,16},{16,24},{24,32},{32,40},{40,48},{48,56},{56,64},{64,7... | collective-permute-start | bytes 294920 | tf_op jit(solution)/shard_map/ppermute | solution.py:62
  372.4 6.9 %collective-permute-start.23 = (bf16[1,22,3,512]{3,2,1,0:T(4,128)(2,1)S(1)}, bf16[1,22,3,512]{3,2,1,0:T(4,128)(2,1)S(1)}, u32[]{:S(2)}, u32[]{:S(2)}) collective-permute-start(bf16[1,22,3,512]{3,2,1,0:T(4,128)(2,1)S(1)} %get-tuple-element.196), channel_id=1, source_target_pairs={{2,0},{4,2},{6,4},{3,1},{5,3},{7,5},{10,8},{12,10},{14,12},{11,9},... | collective-permute-start | bytes 202760 | tf_op jit(solution)/shard_map/ppermute | solution.py:65
  382.4 27.6 %collective-permute-start.27 = (bf16[256,2,1024]{2,0,1:T(8,128)(2,1)}, bf16[256,2,1024]{2,0,1:T(8,128)(2,1)}, u32[]{:S(2)}, u32[]{:S(2)}) collective-permute-start(bf16[256,2,1024]{2,0,1:T(8,128)(2,1)} %bitcast.370), channel_id=1, source_target_pairs={{0,8},{8,0},{1,9},{9,1},{2,10},{10,2},{3,11},{11,3},{4,12},{12,4},... | collective-permute-start | bytes 3145736 | tf_op jit(solution)/shard_map/ppermute | solution.py:28
  383.9 23.3 %all-to-all-start.5 = ((f32[128,1,512]{2,1,0:T(1,128)}), f32[128,1,512]{2,1,0:T(1,128)S(1)}, u32[]{:S(2)}, u32[]{:S(2)}) async-start(f32[128,1,512]{2,1,0:T(1,128)} %stack.794), calls=%async_computation.5 | async-start | bytes 524288 | tf_op jit(solution)/shard_map/all_to_all | solution.py:15
  396.7 13.3 %collective-permute-start.25 = (bf16[256,2,1024]{2,0,1:T(8,128)(2,1)}, bf16[256,2,1024]{2,0,1:T(8,128)(2,1)}, u32[]{:S(2)}, u32[]{:S(2)}) collective-permute-start(bf16[256,2,1024]{2,0,1:T(8,128)(2,1)} %bitcast.371), channel_id=1, source_target_pairs={{0,8},{8,0},{1,9},{9,1},{2,10},{10,2},{3,11},{11,3},{4,12},{12,4},... | collective-permute-start | bytes 3145736 | tf_op jit(solution)/shard_map/ppermute | solution.py:28
  (130 other events, 1645.4 us)
